TPU v7x, 32 devices: a whole 2x2x4 slice. The times are simulated.
32 devices in a mesh: dp: 4 (over x, core), seq: 4 (over z), tensor: 2 (over y).
Axes of the slice: x: 2, y: 2, z: 4, core: 2. Of those that a mesh axis runs over, the one named last changes fastest.
Arguments:
- vit_out: bfloat16 [4096, 3200], P(('dp', 'seq')), may hold values from -6 to 6
- ln_gain: float32 [3200], replicated, may hold values from 0.1 to 1.9
- ln_bias: float32 [3200], replicated, may hold values from -3 to 3
- proj_weight: bfloat16 [3200, 4, 2048], P(None, None, 'tensor'), may hold values from -0.109375 to 0.109375
- proj_bias: float32 [4, 2048], P(None, 'tensor'), may hold values from -3 to 3
- text_embed: bfloat16 [16384, 8192], P('dp', ('seq', 'tensor')), may hold values from -6 to 6
- norm_gain: float32 [8192], P(('seq', 'tensor')), may hold values from 0.1 to 1.9
- tile_dest: int32 [32, 1], replicated, may hold values from 0 to 3; in each aligned block of 8 rows (0 to 7, 8 to 15, ...) at most 4 rows name the same one
- tile_place: int32 [4, 32], replicated, may hold values from 0 to 31, each once within a row
Outputs:
- normed: bfloat16 [16384, 8192], P('dp', ('seq', 'tensor'))
Inputs may be any that keep to these rules, and one draw needn't show every extreme that they name: `tile_dest`: in each aligned block of 8 rows (one encoder group's tiles) no replica is named more than 4 times, a bound that some block reaches. `tile_place`: each row is a permutation of 0 to 31.
All inputs are finite; a program needn't handle non-finite values.
Results may differ from a plain program's by a relative error of at most 0.0048.
Values may be sent and summed in bfloat16 or wider, within the bound.
A program may use at most 128 MiB of HBM per device.

v0:
```python
import jax
import jax.numpy as jnp
from jax import lax
from jax.sharding import PartitionSpec as P

D = 8192
TILE = 128


def layer_norm(rows, ln_gain, ln_bias):
    values = rows.astype(jnp.float32)
    center = values - jnp.mean(values, axis=-1, keepdims=True)
    spread = jnp.mean(center * center, axis=-1, keepdims=True)
    return (center * lax.rsqrt(spread + 1e-06) * ln_gain + ln_bias).astype(jnp.bfloat16)


def arrival_ranks(destination, replicas):
    onehot = (destination[:, None] == jnp.arange(replicas, dtype=jnp.int32)[None, :]).astype(
        jnp.int32
    )
    before = jnp.cumsum(onehot, axis=0) - onehot
    return jnp.sum(before * onehot, axis=1)


def row_squares(rows):
    values = rows.astype(jnp.float32)
    return jnp.sum(values * values, axis=-1)


def local(
    vit_out, ln_gain, ln_bias, proj_weight, proj_bias, text_embed, norm_gain, tile_dest, tile_place
):
    replicas = lax.axis_size("dp")
    owners = lax.axis_size("seq")
    my_replica = lax.axis_index("dp")
    local_rows = vit_out.shape[0]
    width_in = vit_out.shape[1]
    column_block = proj_weight.shape[2]
    positions = tile_place.shape[1]
    seq_rows = text_embed.shape[0]
    group_tiles = owners * local_rows // TILE
    total_tiles = tile_dest.shape[0]
    normed_in = layer_norm(vit_out, ln_gain, ln_bias)
    weights_flat = proj_weight.reshape(width_in, owners * column_block)
    hidden = jnp.dot(
        normed_in, weights_flat, preferred_element_type=jnp.float32
    ) + proj_bias.reshape(-1)
    projected = hidden.astype(jnp.bfloat16)
    regrouped = lax.all_to_all(
        projected.reshape(local_rows, owners, column_block),
        "seq",
        split_axis=1,
        concat_axis=0,
        tiled=True,
    )
    group_rows = regrouped.reshape(owners * local_rows, column_block)
    destination = tile_dest[:, 0]
    ranks = arrival_ranks(destination, replicas)
    place_row = lax.dynamic_index_in_dim(tile_place, my_replica, 0, keepdims=False)
    slot_of_tile = jnp.where(
        destination == my_replica, jnp.take(place_row, jnp.minimum(ranks, positions - 1)), -1
    )
    matches = slot_of_tile[None, :] == jnp.arange(positions, dtype=jnp.int32)[:, None]
    source_tile = (
        jnp.sum(
            matches.astype(jnp.int32) * (jnp.arange(total_tiles, dtype=jnp.int32) + 1)[None, :],
            axis=1,
        )
        - 1
    )
    text_tiles = text_embed.reshape(positions, TILE, column_block)
    capacity = max(2, 2 * group_tiles // replicas)
    local_dest = lax.dynamic_slice_in_dim(destination, my_replica * group_tiles, group_tiles)
    local_rank = arrival_ranks(local_dest, replicas)
    slot_index = local_dest * capacity + local_rank
    filling = slot_index[None, :] == jnp.arange(replicas * capacity, dtype=jnp.int32)[:, None]
    slot_source = (
        jnp.sum(
            filling.astype(jnp.int32) * (jnp.arange(group_tiles, dtype=jnp.int32) + 1)[None, :],
            axis=1,
        )
        - 1
    )
    tiles = group_rows.reshape(group_tiles, TILE, column_block)
    outgoing = jnp.where(
        (slot_source >= 0)[:, None, None],
        tiles[jnp.clip(slot_source, 0, group_tiles - 1)],
        jnp.zeros((), jnp.bfloat16),
    )
    outgoing = outgoing.reshape(replicas, capacity, TILE, column_block)
    incoming = lax.all_to_all(outgoing, "dp", split_axis=0, concat_axis=0, tiled=True).reshape(
        replicas * capacity, TILE, column_block
    )
    group_ranks = jax.vmap(lambda block: arrival_ranks(block, replicas))(
        destination.reshape(replicas, group_tiles)
    ).reshape(-1)
    safe_tile = jnp.clip(source_tile, 0, total_tiles - 1)
    arrival_index = safe_tile // group_tiles * capacity + jnp.take(group_ranks, safe_tile)
    picked = incoming[jnp.clip(arrival_index, 0, replicas * capacity - 1)]
    assembled = jnp.where((source_tile >= 0)[:, None, None], picked, text_tiles).reshape(
        seq_rows, column_block
    )
    squares = row_squares(assembled)
    totals = lax.psum(squares, ("seq", "tensor"))
    scale = lax.rsqrt(totals / D + 1e-05)
    return (assembled.astype(jnp.float32) * scale[:, None] * norm_gain).astype(jnp.bfloat16)


def solution(mesh):
    placed = (
        P(("dp", "seq"), None),
        P(),
        P(),
        P(None, None, "tensor"),
        P(None, "tensor"),
        P("dp", ("seq", "tensor")),
        P(("seq", "tensor")),
        P(),
        P(),
    )
    return jax.shard_map(
        local, mesh=mesh, in_specs=placed, out_specs=P("dp", ("seq", "tensor")), check_vma=False
    )
```

profile of v0, /device:TPU:0, one launch (start us, length us, event | category | flops | bytes accessed | tf_op | source)
XLA Modules:
  0.0 208.5 jit_solution(405158420390305600)
XLA Ops:
  0.0 18.2 %copy.13 = bf16[400,8,4,1024]{3,1,2,0:T(8,128)(2,1)} copy(bf16[400,8,4,1024]{3,2,1,0:T(4,128)(2,1)} %bitcast.39) | data formatting | bytes 52428800
  18.3 0.3 convert_reduce_fusion
  18.6 0.6 fusion.6
  19.2 12.3 %fusion.3 = bf16[256,4096]{1,0:T(8,128)(2,1)S(1)} fusion(bf16[3200,4096]{1,0:T(8,128)(2,1)} %bitcast.40, f32[4096]{0:T(1024)S(1)} %bitcast.46, bf16[256,3200]{1,0:T(8,128)(2,1)S(1)} %copy-done.1, f32[3200]{0:T(1024)S(1)} %copy-done.5, f32[3200]{0:T(1024)S(1)} %copy-done.6, f32[256]{0:T(256)S(1)} %add_rsqrt_fusion.1, f32[256]{0:T(256)S(1)} %broadcast_multiply_fusion), kind=kOutput, calls=%fused_computation.11 | convolution fusion | flops 6717898752 | bytes 29993984 | tf_op jit(solution)/shard_map/dot_general | solution.py:45
  31.5 1.5 copy.17
  33.0 6.4 %all-to-all-start = ((bf16[256,4,1024]{2,0,1:T(8,128)(2,1)}), bf16[256,4,1024]{2,0,1:T(8,128)(2,1)S(1)}, u32[]{:S(2)}, u32[]{:S(2)}) async-start(bf16[256,4,1024]{2,0,1:T(8,128)(2,1)} %bitcast.43), calls=%async_computation | async-start | bytes 4194304 | tf_op jit(solution)/shard_map/all_to_all | solution.py:49
  39.5 0.2 reduce_window_sum.34
  39.8 0.1 select_reduce_fusion.3
  40.0 47.6 %all-to-all-done = bf16[256,4,1024]{2,0,1:T(8,128)(2,1)S(1)} async-done(((bf16[256,4,1024]{2,0,1:T(8,128)(2,1)}), bf16[256,4,1024]{2,0,1:T(8,128)(2,1)S(1)}, u32[]{:S(2)}, u32[]{:S(2)}) %all-to-all-start) | async-done | bytes 2097184 | tf_op jit(solution)/shard_map/all_to_all | solution.py:49
  87.6 2.8 %gather_fusion = bf16[16,128,1024]{2,1,0:T(8,128)(2,1)} fusion(bf16[8,128,1024]{2,1,0:T(8,128)(2,1)S(1)} %bitcast.41, s32[1024]{0:T(1024)S(1)} %pad_clamp_fusion.2), kind=kCustom, calls=%fused_computation.2 | custom fusion | bytes 8388672 | tf_op jit(solution)/shard_map/gather | solution.py:87
  90.4 4.5 %broadcast_select_fusion = bf16[4,4,128,1024]{3,2,1,0:T(8,128)(2,1)} fusion(bf16[4,4,128,1024]{3,2,1,0:T(8,128)(2,1)} %bitcast.42, pred[4,4]{1,0:T(4,128)(4,1)S(1)} %ge.24), kind=kLoop, calls=%fused_computation.12 | loop fusion | flops 2097152 | bytes 8388624 | tf_op jit(solution)/shard_map/jit(_where)/select_n | solution.py:85
  95.0 4.9 %all-to-all-start.1 = ((bf16[4,4,128,1024]{3,2,1,0:T(8,128)(2,1)}), bf16[4,4,128,1024]{3,2,1,0:T(8,128)(2,1)}, u32[]{:S(2)}, u32[]{:S(2)}) async-start(bf16[4,4,128,1024]{3,2,1,0:T(8,128)(2,1)} %broadcast_select_fusion), calls=%async_computation.1 | async-start | bytes 8388608 | tf_op jit(solution)/shard_map/all_to_all | solution.py:91
  99.9 0.6 broadcast.200
  100.5 0.7 reduce.3
  101.3 0.7 reduce_window_sum.35
  102.3 0.2 select_reduce_fusion.1
  102.5 0.7 gather_fusion.2
  103.2 0.1 select_reduce_fusion
  103.3 0.7 gather_fusion.3
  104.1 43.9 %all-to-all-done.1 = bf16[4,4,128,1024]{3,2,1,0:T(8,128)(2,1)} async-done(((bf16[4,4,128,1024]{3,2,1,0:T(8,128)(2,1)}), bf16[4,4,128,1024]{3,2,1,0:T(8,128)(2,1)}, u32[]{:S(2)}, u32[]{:S(2)}) %all-to-all-start.1) | async-done | bytes 4194336 | tf_op jit(solution)/shard_map/all_to_all | solution.py:91
  148.1 7.1 %gather_fusion.1 = bf16[32,128,1024]{2,1,0:T(8,128)(2,1)} fusion(bf16[16,128,1024]{2,1,0:T(8,128)(2,1)} %bitcast.10, s32[1024]{0:T(1024)S(1)} %pad_clamp_fusion), kind=kCustom, calls=%fused_computation.3 | custom fusion | bytes 16777344 | tf_op jit(solution)/shard_map/gather | solution.py:99
  155.2 7.7 %fusion = f32[4096]{0:T(1024)S(1)} fusion(bf16[4096,1024]{1,0:T(8,128)(2,1)} %param.16, bf16[32,128,1024]{2,1,0:T(8,128)(2,1)} %gather_fusion.1, pred[4096]{0:T(1024)(128)(4,1)S(1)} %broadcast_bitcast_fusion), kind=kLoop, calls=%fused_computation.6 | loop fusion | flops 16773120 | bytes 16797696 | tf_op jit(solution)/shard_map/reduce_sum | solution.py:27
  162.9 35.3 %psum.7 = f32[4096]{0:T(1024)S(1)} all-reduce(f32[4096]{0:T(1024)S(1)} %fusion), channel_id=1, replica_groups=mesh['dp'=4,'seq'=4,'tensor'=2] {'seq','tensor'}, use_global_device_ids=true, to_apply=%region_11.13 | all-reduce | flops 4096 | bytes 32768 | tf_op jit(solution)/shard_map/psum | solution.py:104
  198.2 10.2 %fusion.2 = bf16[4096,1024]{1,0:T(8,128)(2,1)} fusion(f32[1024]{0:T(1024)S(1)} %copy-done.4, f32[4096]{0:T(1024)S(1)} %add_rsqrt_fusion, bf16[4096,1024]{1,0:T(8,128)(2,1)} %param.16, bf16[32,128,1024]{2,1,0:T(8,128)(2,1)} %gather_fusion.1, pred[4096]{0:T(1024)(128)(4,1)S(1)} %broadcast_bitcast_fusion), kind=kLoop, calls=%fused_computation.8 | loop fusion | flops 20971520 | bytes 25190400 | tf_op jit(solution)/shard_map/convert_element_type | solution.py:106
  (42 shorter events, 0.8 us)
Async XLA Ops:
  0.0 102.2 %copy-start = (s32[4,32]{1,0:T(4,128)S(1)}, s32[4,32]{1,0:T(4,128)}, u32[]{:S(2)}) copy-start(s32[4,32]{1,0:T(4,128)} %param.19) | copy-start | bytes 1540
  0.0 18.2 %copy-start.2 = (f32[4,1024]{1,0:T(4,128)S(1)}, f32[4,1024]{1,0:T(4,128)}, u32[]{:S(2)}) copy-start(f32[4,1024]{1,0:T(4,128)} %param.15) | copy-start | bytes 49156
  0.0 18.2 %copy-start.1 = (bf16[256,3200]{1,0:T(8,128)(2,1)S(1)}, bf16[256,3200]{1,0:T(8,128)(2,1)}, u32[]{:S(2)}) copy-start(bf16[256,3200]{1,0:T(8,128)(2,1)} %param.11) | copy-start | bytes 4915204
  0.0 19.1 %copy-start.5 = (f32[3200]{0:T(1024)S(1)}, f32[3200]{0:T(1024)}, u32[]{:S(2)}) copy-start(f32[3200]{0:T(1024)} %param.13) | copy-start | bytes 38404
  0.0 19.2 %copy-start.6 = (f32[3200]{0:T(1024)S(1)}, f32[3200]{0:T(1024)}, u32[]{:S(2)}) copy-start(f32[3200]{0:T(1024)} %param.12) | copy-start | bytes 38404
  31.5 7.9 %copy-start.3 = (s32[32,1]{0,1:T(1,128)S(1)}, s32[32,1]{0,1:T(1,128)}, u32[]{:S(2)}) copy-start(s32[32,1]{0,1:T(1,128)} %param.18) | copy-start | bytes 388
  33.0 54.6 %all-to-all-start = ((bf16[256,4,1024]{2,0,1:T(8,128)(2,1)}), bf16[256,4,1024]{2,0,1:T(8,128)(2,1)S(1)}, u32[]{:S(2)}, u32[]{:S(2)}) async-start(bf16[256,4,1024]{2,0,1:T(8,128)(2,1)} %bitcast.43), calls=%async_computation | async-start | bytes 4194304 | tf_op jit(solution)/shard_map/all_to_all | solution.py:49
  95.0 53.1 %all-to-all-start.1 = ((bf16[4,4,128,1024]{3,2,1,0:T(8,128)(2,1)}), bf16[4,4,128,1024]{3,2,1,0:T(8,128)(2,1)}, u32[]{:S(2)}, u32[]{:S(2)}) async-start(bf16[4,4,128,1024]{3,2,1,0:T(8,128)(2,1)} %broadcast_select_fusion), calls=%async_computation.1 | async-start | bytes 8388608 | tf_op jit(solution)/shard_map/all_to_all | solution.py:91
  155.2 43.0 %copy-start.4 = (f32[1024]{0:T(1024)S(1)}, f32[1024]{0:T(1024)}, u32[]{:S(2)}) copy-start(f32[1024]{0:T(1024)} %param.17) | copy-start | bytes 12292
where the time goes:
time: 209 us; the launch traced here: 208 us
  waiting for transfers between devices  91.6 us (44%)
  blocking collectives  35.3 us (17%)
  local copies, waits for them, and re-layouts  32.1 us (15%)
  other arithmetic  25.8 us (12%)
  matrix products  12.3 us (6%)
  starting transfers between devices  11.3 us (5%)
    all_to_all x1, waiting for transfers between devices, local(): lax.all_to_all(projected.reshape(local_rows, owners, column_block), 'seq'...  47.6 us
    all_to_all x1, waiting for transfers between devices, local(): lax.all_to_all(outgoing, 'dp', split_axis=0, concat_axis=0, tiled=True)  43.9 us
    psum x1, blocking collectives, local(): totals = lax.psum(squares, ('seq', 'tensor'))  35.3 us
    unnamed x17, local copies, waits for them, and re-layouts  18.8 us
    dot_general x1, matrix products, local(): jnp.dot(normed_in, weights_flat, preferred_element_type=jnp.float32)  12.3 us
    convert_element_type x1, other arithmetic, local(): (assembled.astype(jnp.float32) * scale[:, None] * norm_gain).astype(jnp.b...  10.2 us
    reduce_sum x1, other arithmetic, row_squares(): return jnp.sum(values * values, axis=-1)  7.74 us
    gather x1, local copies, waits for them, and re-layouts, local(): picked = incoming[jnp.clip(arrival_index, 0, replicas * capacity - 1)]  7.11 us
  transfers between devices with their start and end apart: 2, of which 2 were waited for; matrix products, arithmetic and copies ran while one was open for 2% of the time, Pallas kernels for 0%

commit v1 on v0

--- a/solution.py
+++ b/solution.py
@@ -46,13 +46,11 @@
         normed_in, weights_flat, preferred_element_type=jnp.float32
     ) + proj_bias.reshape(-1)
     projected = hidden.astype(jnp.bfloat16)
-    regrouped = lax.all_to_all(
-        projected.reshape(local_rows, owners, column_block),
-        "seq",
-        split_axis=1,
-        concat_axis=0,
-        tiled=True,
-    )
+    block_2 = projected.reshape(local_rows, owners, column_block)
+    size = lax.axis_size("seq")
+    tiles_2 = jnp.stack(jnp.split(block_2, size, axis=1), axis=0)
+    tiles_2 = lax.all_to_all(tiles_2, "seq", split_axis=0, concat_axis=0)
+    regrouped = jnp.concatenate(tiles_2, axis=0)
     group_rows = regrouped.reshape(owners * local_rows, column_block)
     destination = tile_dest[:, 0]
     ranks = arrival_ranks(destination, replicas)

time: 209 us -> 217 us (1.038)
  local copies, waits for them, and re-layouts: 32.1 us -> 37.7 us
    split x0 -> x1, local copies, waits for them, and re-layouts: none -> 3.05 us  [local(): tiles_2 = jnp.stack(jnp.split(block_2, size, axis=1), axis=0)]
where the time goes in v1:
time: 217 us
  waiting for transfers between devices  91.6 us (42%)
  local copies, waits for them, and re-layouts  37.7 us (17%)
  blocking collectives  35.3 us (16%)
  other arithmetic  27.3 us (13%)
  matrix products  13.3 us (6%)
  starting transfers between devices  11.3 us (5%)
    all_to_all x1, waiting for transfers between devices, local(): tiles_2 = lax.all_to_all(tiles_2, 'seq', split_axis=0, concat_axis=0)  47.6 us
    all_to_all x1, waiting for transfers between devices, local(): lax.all_to_all(outgoing, 'dp', split_axis=0, concat_axis=0, tiled=True)  43.9 us
    psum x1, blocking collectives, local(): totals = lax.psum(squares, ('seq', 'tensor'))  35.3 us
    unnamed x17, local copies, waits for them, and re-layouts  18.8 us
    dot_general x1, matrix products, local(): jnp.dot(normed_in, weights_flat, preferred_element_type=jnp.float32)  13.3 us
    convert_element_type x1, other arithmetic, local(): (assembled.astype(jnp.float32) * scale[:, None] * norm_gain).astype(jnp.b...  10.2 us
    reduce_sum x1, other arithmetic, row_squares(): return jnp.sum(values * values, axis=-1)  7.74 us
    gather x1, local copies, waits for them, and re-layouts, local(): picked = incoming[jnp.clip(arrival_index, 0, replicas * capacity - 1)]  7.11 us
  transfers between devices with their start and end apart: 2, of which 2 were waited for; matrix products, arithmetic and copies ran while one was open for 2% of the time, Pallas kernels for 0%

profile of v1, /device:TPU:0, one launch (start us, length us, event | category | flops | bytes accessed | tf_op | source)
XLA Modules:
  0.0 216.7 jit_solution(1969978950770498820)
XLA Ops:
  0.0 18.2 %copy.25 = bf16[400,8,4,1024]{3,1,2,0:T(8,128)(2,1)} copy(bf16[400,8,4,1024]{3,2,1,0:T(4,128)(2,1)} %bitcast.39) | data formatting | bytes 52428800
  18.3 0.3 convert_reduce_fusion
  18.6 0.6 fusion.6
  19.2 13.3 %fusion.3 = bf16[256,4096]{1,0:T(8,128)(2,1)} fusion(bf16[3200,4096]{1,0:T(8,128)(2,1)} %bitcast.40, f32[4096]{0:T(1024)S(1)} %bitcast.44, bf16[256,3200]{1,0:T(8,128)(2,1)S(1)} %copy-done.1, f32[3200]{0:T(1024)S(1)} %copy-done.5, f32[3200]{0:T(1024)S(1)} %copy-done.6, f32[256]{0:T(256)S(1)} %add_rsqrt_fusion.1, f32[256]{0:T(256)S(1)} %broadcast_multiply_fusion), kind=kOutput, calls=%fused_computation.11 | convolution fusion | flops 6717898752 | bytes 29993984 | tf_op jit(solution)/shard_map/dot_general | solution.py:45
  32.5 3.3 %reshape.100 = bf16[256,4,1024]{2,1,0:T(4,128)(2,1)S(1)} reshape(bf16[256,4096]{1,0:T(8,128)(2,1)} %fusion.3) | data formatting | bytes 4194304 | tf_op jit(solution)/shard_map/reshape | solution.py:49
  35.8 3.1 %fusion.20 = (bf16[256,1,1024]{2,1,0:T(2,128)(2,1)S(1)}, bf16[256,1,1024]{2,1,0:T(2,128)(2,1)S(1)}, bf16[256,1,1024]{2,1,0:T(2,128)(2,1)S(1)}, bf16[256,1,1024]{2,1,0:T(2,128)(2,1)S(1)}) fusion(bf16[256,4,1024]{2,1,0:T(4,128)(2,1)S(1)} %reshape.100), kind=kLoop, calls=%fused_computation.73 | loop fusion | bytes 4194304 | tf_op jit(solution)/shard_map/split | solution.py:51
  38.9 0.4 copy_bitcast_fusion
  39.2 0.4 copy_bitcast_fusion.2
  39.6 1.6 pad_maximum_fusion
  41.2 6.4 %all-to-all-start = ((bf16[4,256,1,1024]{3,1,2,0:T(8,128)(2,1)}), bf16[4,256,1,1024]{3,1,2,0:T(8,128)(2,1)S(1)}, u32[]{:S(2)}, u32[]{:S(2)}) async-start(bf16[4,256,1,1024]{3,1,2,0:T(8,128)(2,1)} %pad_maximum_fusion), calls=%async_computation | async-start | bytes 4194304 | tf_op jit(solution)/shard_map/all_to_all | solution.py:52
  48.2 47.6 %all-to-all-done = bf16[4,256,1,1024]{3,1,2,0:T(8,128)(2,1)S(1)} async-done(((bf16[4,256,1,1024]{3,1,2,0:T(8,128)(2,1)}), bf16[4,256,1,1024]{3,1,2,0:T(8,128)(2,1)S(1)}, u32[]{:S(2)}, u32[]{:S(2)}) %all-to-all-start) | async-done | bytes 2097184 | tf_op jit(solution)/shard_map/all_to_all | solution.py:52
  95.8 2.8 %gather_fusion = bf16[16,128,1024]{2,1,0:T(8,128)(2,1)} fusion(bf16[8,128,1024]{2,1,0:T(8,128)(2,1)S(1)} %bitcast.41, s32[1024]{0:T(1024)S(1)} %pad_clamp_fusion.2), kind=kCustom, calls=%fused_computation.2 | custom fusion | bytes 8388672 | tf_op jit(solution)/shard_map/gather | solution.py:85
  98.6 4.5 %broadcast_select_fusion = bf16[4,4,128,1024]{3,2,1,0:T(8,128)(2,1)} fusion(bf16[4,4,128,1024]{3,2,1,0:T(8,128)(2,1)} %bitcast.42, pred[4,4]{1,0:T(4,128)(4,1)S(1)} %ge.24), kind=kLoop, calls=%fused_computation.12 | loop fusion | flops 2097152 | bytes 8388624 | tf_op jit(solution)/shard_map/jit(_where)/select_n | solution.py:83
  103.2 4.9 %all-to-all-start.1 = ((bf16[4,4,128,1024]{3,2,1,0:T(8,128)(2,1)}), bf16[4,4,128,1024]{3,2,1,0:T(8,128)(2,1)}, u32[]{:S(2)}, u32[]{:S(2)}) async-start(bf16[4,4,128,1024]{3,2,1,0:T(8,128)(2,1)} %broadcast_select_fusion), calls=%async_computation.1 | async-start | bytes 8388608 | tf_op jit(solution)/shard_map/all_to_all | solution.py:89
  108.1 0.6 broadcast.200
  108.7 0.7 reduce.3
  109.5 0.7 reduce_window_sum.35
  110.7 0.7 gather_fusion.2
  111.5 0.7 gather_fusion.3
  112.3 43.9 %all-to-all-done.1 = bf16[4,4,128,1024]{3,2,1,0:T(8,128)(2,1)} async-done(((bf16[4,4,128,1024]{3,2,1,0:T(8,128)(2,1)}), bf16[4,4,128,1024]{3,2,1,0:T(8,128)(2,1)}, u32[]{:S(2)}, u32[]{:S(2)}) %all-to-all-start.1) | async-done | bytes 4194336 | tf_op jit(solution)/shard_map/all_to_all | solution.py:89
  156.3 7.1 %gather_fusion.1 = bf16[32,128,1024]{2,1,0:T(8,128)(2,1)} fusion(bf16[16,128,1024]{2,1,0:T(8,128)(2,1)} %bitcast.12, s32[1024]{0:T(1024)S(1)} %pad_clamp_fusion), kind=kCustom, calls=%fused_computation.3 | custom fusion | bytes 16777344 | tf_op jit(solution)/shard_map/gather | solution.py:97
  163.4 7.7 %fusion = f32[4096]{0:T(1024)S(1)} fusion(bf16[4096,1024]{1,0:T(8,128)(2,1)} %param.16, bf16[32,128,1024]{2,1,0:T(8,128)(2,1)} %gather_fusion.1, pred[4096]{0:T(1024)(128)(4,1)S(1)} %broadcast_bitcast_fusion), kind=kLoop, calls=%fused_computation.6 | loop fusion | flops 16773120 | bytes 16797696 | tf_op jit(solution)/shard_map/reduce_sum | solution.py:27
  171.1 35.3 %psum.7 = f32[4096]{0:T(1024)S(1)} all-reduce(f32[4096]{0:T(1024)S(1)} %fusion), channel_id=1, replica_groups=mesh['dp'=4,'seq'=4,'tensor'=2] {'seq','tensor'}, use_global_device_ids=true, to_apply=%region_11.13 | all-reduce | flops 4096 | bytes 32768 | tf_op jit(solution)/shard_map/psum | solution.py:102
  206.4 10.2 %fusion.2 = bf16[4096,1024]{1,0:T(8,128)(2,1)} fusion(f32[1024]{0:T(1024)S(1)} %copy-done.4, f32[4096]{0:T(1024)S(1)} %add_rsqrt_fusion, bf16[4096,1024]{1,0:T(8,128)(2,1)} %param.16, bf16[32,128,1024]{2,1,0:T(8,128)(2,1)} %gather_fusion.1, pred[4096]{0:T(1024)(128)(4,1)S(1)} %broadcast_bitcast_fusion), kind=kLoop, calls=%fused_computation.8 | loop fusion | flops 20971520 | bytes 25190400 | tf_op jit(solution)/shard_map/convert_element_type | solution.py:104
  (46 shorter events, 1.4 us)
Async XLA Ops:
  0.0 110.4 %copy-start = (s32[4,32]{1,0:T(4,128)S(1)}, s32[4,32]{1,0:T(4,128)}, u32[]{:S(2)}) copy-start(s32[4,32]{1,0:T(4,128)} %param.19) | copy-start | bytes 1540
  0.0 18.2 %copy-start.2 = (f32[4,1024]{1,0:T(4,128)S(1)}, f32[4,1024]{1,0:T(4,128)}, u32[]{:S(2)}) copy-start(f32[4,1024]{1,0:T(4,128)} %param.15) | copy-start | bytes 49156
  0.0 18.2 %copy-start.1 = (bf16[256,3200]{1,0:T(8,128)(2,1)S(1)}, bf16[256,3200]{1,0:T(8,128)(2,1)}, u32[]{:S(2)}) copy-start(bf16[256,3200]{1,0:T(8,128)(2,1)} %param.11) | copy-start | bytes 4915204
  0.0 19.1 %copy-start.5 = (f32[3200]{0:T(1024)S(1)}, f32[3200]{0:T(1024)}, u32[]{:S(2)}) copy-start(f32[3200]{0:T(1024)} %param.13) | copy-start | bytes 38404
  0.0 19.2 %copy-start.6 = (f32[3200]{0:T(1024)S(1)}, f32[3200]{0:T(1024)}, u32[]{:S(2)}) copy-start(f32[3200]{0:T(1024)} %param.12) | copy-start | bytes 38404
  39.6 8.0 %copy-start.3 = (s32[32,1]{0,1:T(1,128)S(1)}, s32[32,1]{0,1:T(1,128)}, u32[]{:S(2)}) copy-start(s32[32,1]{0,1:T(1,128)} %param.18) | copy-start | bytes 388
  41.2 54.6 %all-to-all-start = ((bf16[4,256,1,1024]{3,1,2,0:T(8,128)(2,1)}), bf16[4,256,1,1024]{3,1,2,0:T(8,128)(2,1)S(1)}, u32[]{:S(2)}, u32[]{:S(2)}) async-start(bf16[4,256,1,1024]{3,1,2,0:T(8,128)(2,1)} %pad_maximum_fusion), calls=%async_computation | async-start | bytes 4194304 | tf_op jit(solution)/shard_map/all_to_all | solution.py:52
  103.2 53.1 %all-to-all-start.1 = ((bf16[4,4,128,1024]{3,2,1,0:T(8,128)(2,1)}), bf16[4,4,128,1024]{3,2,1,0:T(8,128)(2,1)}, u32[]{:S(2)}, u32[]{:S(2)}) async-start(bf16[4,4,128,1024]{3,2,1,0:T(8,128)(2,1)} %broadcast_select_fusion), calls=%async_computation.1 | async-start | bytes 8388608 | tf_op jit(solution)/shard_map/all_to_all | solution.py:89
  163.4 43.0 %copy-start.4 = (f32[1024]{0:T(1024)S(1)}, f32[1024]{0:T(1024)}, u32[]{:S(2)}) copy-start(f32[1024]{0:T(1024)} %param.17) | copy-start | bytes 12292
